TPU v7x, 256 devices: a whole 4x4x8 slice. The times are simulated.
256 devices in a mesh: expert: 16 (over x, y), dp: 16 (over z, core).
Axes of the slice: x: 4, y: 4, z: 8, core: 2. Of those that a mesh axis runs over, the one named last changes fastest.
Arguments:
- tokens: bfloat16 [2, 32768, 1280], P(None, ('expert', 'dp')), may hold values from -6 to 6
- modality: int32 [2, 32768], P(None, ('expert', 'dp')), may hold values from 0 to 1, as said below
- routes: int32 [2, 32768, 1], P(None, ('expert', 'dp')), may hold values from 0 to 15; in each aligned block of 128 rows (0 to 127, 128 to 255, ..., all dimensions but the last counted through in order) at most 16 rows name the same one
- router: bfloat16 [1280, 16], replicated, may hold values from -0.15625 to 0.15625
- w_in: bfloat16 [16, 1280, 5120], P('expert', 'dp'), may hold values from -0.15625 to 0.15625
- w_out: bfloat16 [16, 5120, 1280], P('expert', 'dp'), may hold values from -0.078125 to 0.078125
Outputs:
- mixed: bfloat16 [2, 32768, 1280], P(None, ('expert', 'dp'))
- load: float32 [2, 2, 16], replicated
Inputs may be any that keep to these rules, and one draw needn't show every extreme that they name: `routes`: among the 128 tokens of one micro-batch on one device (aligned blocks of 128 rows), at most 16 are routed to any one expert. `modality`: in every aligned block of 128 tokens of a micro-batch, the number of text tokens lies between 32 and 96.
All inputs are finite; a program needn't handle non-finite values.
Results may differ from a plain program's by a relative error of at most 0.0057.
Values may be sent and summed in bfloat16 or wider, within the bound.
A program may use at most 192 MiB of HBM per device.

v0:
```python
import jax
import jax.numpy as jnp
from jax import lax
from jax.sharding import Mesh
from jax.sharding import PartitionSpec as P

EXPERT = ("expert_0", "expert_1")
DP = ("dp_0", "dp_1")
EXPERT_DP = ("expert_0", "expert_1", "dp_0", "dp_1")


def over_axes(shard, axes):
    for axis in axes:
        shard = lax.psum(shard, axis)
    return shard


def on_device(tokens, modality, routes, router, w_in, w_out):
    micro_count, tok_count, model_width = tokens.shape
    experts = router.shape[1]
    capacity = 2 * tok_count // experts
    logits = jnp.einsum("mtd,de->mte", tokens, router, preferred_element_type=jnp.float32)
    onehot = (routes == jnp.arange(experts, dtype=jnp.int32)[None, None, :]).astype(jnp.float32)
    gating = jax.nn.sigmoid(jnp.sum(logits * onehot, axis=-1))
    running = jnp.cumsum(onehot, axis=1)
    slot_pos = jnp.sum((running - 1.0) * onehot, axis=-1)
    slot_hot = (
        slot_pos[:, :, None] == jnp.arange(capacity, dtype=jnp.float32)[None, None, :]
    ).astype(jnp.float32)
    placer = (onehot[:, :, :, None] * slot_hot[:, :, None, :]).reshape(
        micro_count, tok_count, experts * capacity
    )
    placer = placer.astype(jnp.bfloat16)
    buffer = jnp.einsum("mtk,mtd->mkd", placer, tokens, preferred_element_type=jnp.float32)
    buffer = buffer.astype(jnp.bfloat16).reshape(micro_count, experts, capacity, model_width)
    arrived = lax.all_to_all(buffer, EXPERT, split_axis=1, concat_axis=1, tiled=True)
    token_rows = arrived.reshape(-1, model_width)
    columns = token_rows
    pre_act = jnp.dot(
        columns, lax.all_gather(w_in, DP, axis=1, tiled=True)[0], preferred_element_type=jnp.float32
    )
    hidden = jax.nn.gelu(pre_act, approximate=True).astype(jnp.bfloat16)
    columns = hidden
    served = jnp.dot(
        columns,
        lax.all_gather(w_out, DP, axis=1, tiled=True)[0],
        preferred_element_type=jnp.float32,
    )
    served = served.astype(jnp.bfloat16).reshape(arrived.shape)
    returned = lax.all_to_all(served, EXPERT, split_axis=1, concat_axis=1, tiled=True)
    returned = returned.reshape(micro_count, experts * capacity, model_width)
    combined = jnp.einsum("mtk,mkd->mtd", placer, returned, preferred_element_type=jnp.float32)
    mixed = (combined * gating[:, :, None]).astype(jnp.bfloat16)
    exps = jnp.exp(logits)
    router_probs = exps / jnp.sum(exps, axis=-1, keepdims=True)
    modal_hot = (modality[:, :, None] == jnp.arange(2, dtype=jnp.int32)[None, None, :]).astype(
        jnp.float32
    )
    counts = jnp.einsum("mtk,mte->ke", modal_hot, onehot, precision=lax.Precision.HIGHEST)
    prob_sums = jnp.einsum("mtk,mte->ke", modal_hot, router_probs, precision=lax.Precision.HIGHEST)
    modal_counts = jnp.sum(modal_hot, axis=(0, 1))
    counts, prob_sums, modal_counts = (
        over_axes(counts, EXPERT_DP),
        over_axes(prob_sums, EXPERT_DP),
        over_axes(modal_counts, EXPERT_DP),
    )
    load = jnp.stack(
        [experts * counts / modal_counts[:, None], experts * prob_sums / modal_counts[:, None]]
    )
    return (mixed, load)


def solution(mesh):
    torus = Mesh(mesh.devices.reshape(4, 4, 8, 2), ("expert_0", "expert_1", "dp_0", "dp_1"))
    in_specs = (
        P(None, EXPERT_DP, None),
        P(None, EXPERT_DP),
        P(None, EXPERT_DP, None),
        P(),
        P(EXPERT, DP, None),
        P(EXPERT, DP, None),
    )
    out_specs = (P(None, EXPERT_DP, None), P())
    return jax.shard_map(
        on_device, mesh=torus, in_specs=in_specs, out_specs=out_specs, check_vma=False
    )
```

profile of v0, /device:TPU:1, one launch (start us, length us, event | category | flops | bytes accessed | tf_op | source)
XLA Modules:
  0.0 258.7 jit_solution(4837752513307506845)
XLA Ops:
  7.2 0.0 copy-start
  7.2 0.0 all-gather.5.cloned.1.call-start
  7.2 0.7 all-gather.5.cloned.1.call-update
  7.9 0.0 all-gather.3.cloned.1.call-start
  8.0 0.7 all-gather.3.cloned.1.call-update
  8.7 0.7 fusion.30
  9.3 0.1 copy.21
  9.5 0.2 reduce_window_sum.11
  9.6 0.1 copy.22
  9.7 0.8 fusion.29
  10.5 0.5 convolution_convert_fusion
  11.0 0.1 copy.23
  11.1 26.3 %all_to_all.10 = bf16[2,16,16,1280]{3,2,0,1:T(8,128)(2,1)S(1)} all-to-all(bf16[2,16,16,1280]{3,2,0,1:T(8,128)(2,1)S(1)} %copy.23), channel_id=1, replica_groups=mesh['expert_0'=4,'expert_1'=4,'dp_0'=8,'dp_1'=2] {'expert_0','expert_1'}, dimensions={1} | all-to-all | bytes 2621440 | tf_op jit(solution)/shard_map/all_to_all | solution.py:36
  37.5 0.1 copy.24
  37.6 54.6 %all-gather.5.cloned.1.call-done = bf16[1,5120,1280]{2,1,0:T(8,128)(2,1)} async-done(((bf16[1,320,1280]{2,1,0:T(8,128)(2,1)}), bf16[1,5120,1280]{2,1,0:T(8,128)(2,1)}) %all-gather.5.cloned.1.call-update) | async-done | bytes 13107216 | tf_op jit(solution)/shard_map/all_gather | solution.py:46
  92.1 78.5 %all-gather.3.cloned.1.call-done = bf16[1,1280,5120]{2,1,0:T(8,128)(2,1)} async-done(((bf16[1,80,5120]{2,1,0:T(8,128)(2,1)}), bf16[1,1280,5120]{2,1,0:T(8,128)(2,1)}) %all-gather.3.cloned.1.call-update) | async-done | bytes 13107216 | tf_op jit(solution)/shard_map/all_gather | solution.py:40
  170.6 22.4 %fusion.20 = bf16[512,1280]{1,0:T(8,128)(2,1)S(1)} fusion(bf16[1,5120,1280]{2,1,0:T(8,128)(2,1)} %all-gather.5.cloned.1.call-done, bf16[512,1280]{1,0:T(8,128)(2,1)S(1)} %bitcast.41, bf16[1,1280,5120]{2,1,0:T(8,128)(2,1)} %all-gather.3.cloned.1.call-done), kind=kOutput, calls=%fused_computation.17 | convolution fusion | flops 13446021120 | bytes 28835840 | tf_op jit(solution)/shard_map/dot_general | solution.py:44
  193.0 0.0 copy-start.1
  193.0 1.2 copy.25
  194.2 6.5 %all-to-all-start.1 = ((bf16[2,16,16,1280]{3,2,0,1:T(8,128)(2,1)}), bf16[2,16,16,1280]{3,2,0,1:T(8,128)(2,1)S(1)}, u32[]{:S(2)}, u32[]{:S(2)}) async-start(bf16[2,16,16,1280]{3,2,0,1:T(8,128)(2,1)} %copy.25), calls=%async_computation.1 | async-start | bytes 2621440 | tf_op jit(solution)/shard_map/all_to_all | solution.py:50
  200.8 0.1 convert_reduce_fusion
  200.9 0.1 convolution_bitcast_fusion.1
  201.0 0.3 exponential_reduce_fusion
  201.4 0.1 convolution_bitcast_fusion
  201.5 18.4 %all-reduce.2 = (f32[2,16]{1,0:T(2,128)S(1)}, f32[2]{0:T(128)S(1)}, f32[2,16]{1,0:T(2,128)S(1)}) all-reduce(f32[2,16]{1,0:T(2,128)S(1)} %convolution_bitcast_fusion, f32[2]{0:T(128)S(1)} %convert_reduce_fusion, f32[2,16]{1,0:T(2,128)S(1)} %convolution_bitcast_fusion.1), channel_id=1, replica_groups=mesh['expert_0'=4,'expert_1'=4,'dp_0'=8,'dp_1'=2] {'expert_0'}, use_global_device_ids=true, to_apply=%region_13.14 | all-reduce | flops 66 | bytes 528 | tf_op jit(solution)/shard_map/psum | solution.py:14
  219.9 8.1 %all-reduce.1 = (f32[2,16]{1,0:T(2,128)S(1)}, f32[2]{0:T(128)S(1)}, f32[2,16]{1,0:T(2,128)S(1)}) all-reduce(f32[2,16]{1,0:T(2,128)S(1)} %get-tuple-element.10, f32[2]{0:T(128)S(1)} %get-tuple-element.11, f32[2,16]{1,0:T(2,128)S(1)} %get-tuple-element.12), channel_id=1, replica_groups=mesh['expert_0'=4,'expert_1'=4,'dp_0'=8,'dp_1'=2] {'expert_1'}, use_global_device_ids=true, to_apply=%region_14.15 | all-reduce | flops 66 | bytes 528 | tf_op jit(solution)/shard_map/psum | solution.py:14
  227.9 11.8 %all-reduce = (f32[2,16]{1,0:T(2,128)S(1)}, f32[2]{0:T(128)S(1)}, f32[2,16]{1,0:T(2,128)S(1)}) all-reduce(f32[2,16]{1,0:T(2,128)S(1)} %get-tuple-element.7, f32[2]{0:T(128)S(1)} %get-tuple-element.8, f32[2,16]{1,0:T(2,128)S(1)} %get-tuple-element.9), channel_id=1, replica_groups=mesh['expert_0'=4,'expert_1'=4,'dp_0'=8,'dp_1'=2] {'dp_0'}, use_global_device_ids=true, to_apply=%region_15.16 | all-reduce | flops 66 | bytes 528 | tf_op jit(solution)/shard_map/psum | solution.py:14
  239.7 10.2 %all-reduce.3 = (f32[2,16]{1,0:T(2,128)S(1)}, f32[2]{0:T(128)S(1)}, f32[2,16]{1,0:T(2,128)S(1)}) all-reduce(f32[2,16]{1,0:T(2,128)S(1)} %get-tuple-element.4, f32[2]{0:T(128)S(1)} %get-tuple-element.5, f32[2,16]{1,0:T(2,128)S(1)} %get-tuple-element.6), channel_id=1, replica_groups=mesh['expert_0'=4,'expert_1'=4,'dp_0'=8,'dp_1'=2] {'dp_1'}, use_global_device_ids=true, to_apply=%region_16.17 | all-reduce | flops 66 | bytes 528 | tf_op jit(solution)/shard_map/psum | solution.py:14
  249.9 0.1 divide_bitcast_fusion.1
  249.9 0.6 pad_maximum_fusion
  250.5 0.1 copy.26
  250.6 1.2 fusion.25
  (9 shorter events, 0.1 us)
Async XLA Ops:
  7.2 3.3 %copy-start = (bf16[2,128,1280]{2,1,0:T(8,128)(2,1)S(1)}, bf16[2,128,1280]{2,1,0:T(8,128)(2,1)}, u32[]{:S(2)}) copy-start(bf16[2,128,1280]{2,1,0:T(8,128)(2,1)} %param.6) | copy-start | bytes 1966084
  7.2 84.9 %all-gather.5.cloned.1.call-start = ((), (), s32[]{:S(2)}) async-start(), calls=%async_computation.3 | async-start | bytes 13926400 | tf_op jit(solution)/shard_map/all_gather | solution.py:46
  7.9 162.7 %all-gather.3.cloned.1.call-start = ((), (), s32[]{:S(2)}) async-start(), calls=%async_computation.2 | async-start | bytes 13926400 | tf_op jit(solution)/shard_map/all_gather | solution.py:40
  193.0 7.8 %copy-start.3 = (s32[2,128]{1,0:T(2,128)S(1)}, s32[2,128]{1,0:T(2,128)}, u32[]{:S(2)}) copy-start(s32[2,128]{1,0:T(2,128)} %param.7) | copy-start | bytes 3076
  193.0 7.9 %copy-start.2 = (s32[2,128,1]{1,2,0:T(1,128)S(1)}, s32[2,128,1]{1,2,0:T(1,128)}, u32[]{:S(2)}) copy-start(s32[2,128,1]{1,2,0:T(1,128)} %param.8) | copy-start | bytes 3076
  193.0 8.0 %copy-start.1 = (bf16[1280,16]{0,1:T(8,128)(2,1)S(1)}, bf16[1280,16]{0,1:T(8,128)(2,1)}, u32[]{:S(2)}) copy-start(bf16[1280,16]{0,1:T(8,128)(2,1)} %param.9) | copy-start | bytes 122884
  194.2 56.3 %all-to-all-start.1 = ((bf16[2,16,16,1280]{3,2,0,1:T(8,128)(2,1)}), bf16[2,16,16,1280]{3,2,0,1:T(8,128)(2,1)S(1)}, u32[]{:S(2)}, u32[]{:S(2)}) async-start(bf16[2,16,16,1280]{3,2,0,1:T(8,128)(2,1)} %copy.25), calls=%async_computation.1 | async-start | bytes 2621440 | tf_op jit(solution)/shard_map/all_to_all | solution.py:50
Sparse Core Ops, SparseCore 0:
  9.8 82.2 all-gather.4
  93.9 76.5 all-gather.2
where the time goes:
time: 259 us
  waiting for transfers between devices  134 us (52%)
  blocking collectives  74.7 us (29%)
  matrix products  24.7 us (10%)
  between operations  14.2 us (5%)
  starting transfers between devices  6.6 us (3%)
    all_gather x1, waiting for transfers between devices, on_device(): lax.all_gather(w_in, DP, axis=1, tiled=True)[0]  78.5 us
    all_gather x1, waiting for transfers between devices, on_device(): lax.all_gather(w_out, DP, axis=1, tiled=True)[0]  54.6 us
    psum x4, blocking collectives, over_axes(): shard = lax.psum(shard, axis)  48.4 us
    all_to_all x1, blocking collectives, on_device(): lax.all_to_all(buffer, EXPERT, split_axis=1, concat_axis=1, tiled=True)  26.3 us
    dot_general x1, matrix products, on_device(): jnp.dot(columns, lax.all_gather(w_out, DP, axis=1, tiled=True)[0], prefer...  22.4 us
    all_to_all x1, starting transfers between devices, on_device(): lax.all_to_all(served, EXPERT, split_axis=1, concat_axis=1, tiled=True)  6.52 us
  transfers between devices with their start and end apart: 3, of which 2 were waited for; matrix products, arithmetic and copies ran while one was open for 2% of the time, Pallas kernels for 0%

commit v1 on v0

v1 whole, which is shorter than its diff:
```python
import functools
import math

import jax
import jax.numpy as jnp
from jax import lax
from jax.experimental import pallas as pl
from jax.experimental.pallas import tpu as pltpu
from jax.sharding import Mesh
from jax.sharding import PartitionSpec as P

NX, NY, NZ, NC = 4, 4, 8, 2
AXES = ("expert_0", "expert_1", "dp_0", "dp_1")
MESH = pl.DeviceIdType.MESH
CHUNKS_IN = 4
CHUNKS_OUT = 5
GELU_C = math.sqrt(2.0 / math.pi)


def gelu(v):
    return 0.5 * v * (1.0 + jnp.tanh(GELU_C * (v + 0.044715 * (v * v * v))))


def layer_kernel(
    tokens_ref, routes_ref, modality_ref, router_ref, w_in_ref, w_out_ref,
    mixed_ref, load_ref,
    win, wout, placer, gate, buffer, rows, hidden, served, returned,
    stat, stat_rx, stat_sum, stat_rx2,
    local_sem, ring_send, ring_recv, pair_send, pair_recv,
    disp_send, disp_recv, back_send, back_recv, stat_send, stat_recv,
):
    shard_in = w_in_ref.shape[1]
    shard_out = w_out_ref.shape[1]
    width = tokens_ref.shape[1]
    toks = tokens_ref.shape[0]
    experts = router_ref.shape[1]
    block = rows.shape[0] // experts
    cols_in = win.shape[2]
    cols_out = wout.shape[2]
    chunks = CHUNKS_IN + CHUNKS_OUT
    dps = NZ * NC

    ex, ey = lax.axis_index("expert_0"), lax.axis_index("expert_1")
    z, c = lax.axis_index("dp_0"), lax.axis_index("dp_1")
    me = ex * NY + ey
    mine = z * NC + c
    up, down = lax.rem(z + 1, NZ), lax.rem(z + NZ - 1, NZ)
    other = 1 - c

    def plane_peer(j):
        p = lax.rem(me + j, experts)
        return p, (p // NY, lax.rem(p, NY), z, c)

    def dp_peer(j):
        p = lax.rem(mine + j, dps)
        return p, (ex, ey, p // NC, lax.rem(p, NC))

    def piece(n, source_z, core, half=None):
        shard = source_z * NC + core
        if n < CHUNKS_IN:
            view = win.at[n, pl.ds(pl.multiple_of(shard * shard_in, 16), shard_in)]
            if half is not None:
                view = win.at[
                    n, pl.ds(pl.multiple_of(shard * shard_in, 16), shard_in),
                    pl.ds(half * (cols_in // 2), cols_in // 2)]
            return view
        if half is None:
            return wout.at[n - CHUNKS_IN, pl.ds(pl.multiple_of(shard * shard_out, 16), shard_out)]
        rows_half = shard_out // 2
        return wout.at[
            n - CHUNKS_IN,
            pl.ds(pl.multiple_of(shard * shard_out + half * rows_half, 16), rows_half)]

    def local_copy(n):
        if n < CHUNKS_IN:
            source = w_in_ref.at[0, :, pl.ds(n * cols_in, cols_in)]
        else:
            source = w_out_ref.at[0, :, pl.ds((n - CHUNKS_IN) * cols_out, cols_out)]
        return pltpu.make_async_copy(source, piece(n, z, c), local_sem.at[n])

    def source_of(direction, hop):
        return lax.rem(z + NZ - hop, NZ) if direction == 0 else lax.rem(z + hop, NZ)

    def ring_copy(n, direction, hop):
        half = direction if hop == NZ // 2 else None
        ref = piece(n, source_of(direction, hop - 1), c, half)
        return pltpu.make_async_remote_copy(
            src_ref=ref, dst_ref=ref,
            send_sem=ring_send.at[n, direction, hop - 1],
            recv_sem=ring_recv.at[n, direction, hop - 1],
            device_id=(ex, ey, up if direction == 0 else down, c), device_id_type=MESH)

    def ring_arrival(n, direction, hop):
        half = direction if hop == NZ // 2 else None
        ref = piece(n, source_of(direction, hop), c, half)
        return pltpu.make_async_remote_copy(
            src_ref=ref, dst_ref=ref,
            send_sem=ring_send.at[n, direction, hop - 1],
            recv_sem=ring_recv.at[n, direction, hop - 1],
            device_id=(ex, ey, up if direction == 0 else down, c), device_id_type=MESH)

    def pair_slots():
        slots = [(0, 0)]
        for hop in range(1, NZ // 2):
            slots += [(0, hop), (1, hop)]
        return slots + [(0, NZ // 2)]

    slot_of = {s: k for k, s in enumerate(pair_slots())}

    def pair_copy(n, direction, hop, core):
        ref = piece(n, source_of(direction, hop), core)
        k = slot_of[(direction, hop)]
        return pltpu.make_async_remote_copy(
            src_ref=ref, dst_ref=ref,
            send_sem=pair_send.at[n, k], recv_sem=pair_recv.at[n, k],
            device_id=(ex, ey, z, other), device_id_type=MESH)

    for n in range(chunks):
        local_copy(n).start()

    barrier = pltpu.get_barrier_semaphore()

    def greet_plane(j, carry):
        _, device = plane_peer(j)
        pl.semaphore_signal(barrier, inc=1, device_id=device, device_id_type=MESH)
        return carry

    def greet_dp(j, carry):
        _, device = dp_peer(j)
        pl.semaphore_signal(barrier, inc=1, device_id=device, device_id_type=MESH)
        return carry

    lax.fori_loop(1, dps, greet_dp, 0)
    lax.fori_loop(1, experts, greet_plane, 0)
    pl.semaphore_wait(barrier, experts + dps - 2)

    def send_own(n):
        local_copy(n).wait()
        for direction in range(2):
            ring_copy(n, direction, 1).start()
        pair_copy(n, 0, 0, c).start()

    send_own(0)

    tok = tokens_ref[...]
    logits = jnp.dot(tok, router_ref[...], preferred_element_type=jnp.float32)
    lane = lax.broadcasted_iota(jnp.int32, (toks, experts), 1)
    onehot = (routes_ref[...] == lane).astype(jnp.float32)
    chosen = jnp.sum(logits * onehot, axis=1, keepdims=True)
    gate[...] = jnp.broadcast_to(1.0 / (1.0 + jnp.exp(-chosen)), gate.shape)
    micro_rows = toks // 2
    row_i = lax.broadcasted_iota(jnp.int32, (toks, toks), 0)
    col_i = lax.broadcasted_iota(jnp.int32, (toks, toks), 1)
    first = jnp.where(row_i >= micro_rows, micro_rows, 0)
    earlier = ((col_i <= row_i) & (col_i >= first)).astype(jnp.bfloat16)
    running = jnp.dot(earlier, onehot.astype(jnp.bfloat16), preferred_element_type=jnp.float32)
    lane_f = lane.astype(jnp.float32)
    spot = jnp.sum((running - 1.0 + lane_f * block) * onehot, axis=1, keepdims=True)
    token_id = lax.broadcasted_iota(jnp.int32, (toks, 1), 0)
    spot = spot + jnp.where(token_id >= micro_rows, block // 2, 0).astype(jnp.float32)
    slots = lax.broadcasted_iota(jnp.int32, (toks, experts * block), 1).astype(jnp.float32)
    place = (spot == slots).astype(jnp.bfloat16)
    placer[...] = place
    buffer[...] = lax.dot_general(
        place, tok, (((0,), (0,)), ((), ())), preferred_element_type=jnp.float32
    ).astype(jnp.bfloat16)

    exps = jnp.exp(logits)
    probs = exps / jnp.sum(exps, axis=1, keepdims=True)
    stat[...] = jnp.zeros(stat.shape, jnp.float32)
    for k in range(2):
        modal = (modality_ref[...] == k).astype(jnp.float32)
        stat[k:k + 1, 0:experts] = jnp.sum(onehot * modal, axis=0, keepdims=True)
        stat[2 + k:3 + k, 0:experts] = jnp.sum(probs * modal, axis=0, keepdims=True)
        stat[4 + k:5 + k, 0:experts] = jnp.sum(
            jnp.broadcast_to(modal, (toks, experts)), axis=0, keepdims=True)

    def dispatch(j, carry):
        p, device = plane_peer(j)
        pltpu.make_async_remote_copy(
            src_ref=buffer.at[pl.ds(pl.multiple_of(p * block, 16), block)],
            dst_ref=rows.at[pl.ds(pl.multiple_of(me * block, 16), block)],
            send_sem=disp_send, recv_sem=disp_recv,
            device_id=device, device_id_type=MESH).start()
        return carry

    own_rows = pl.ds(pl.multiple_of(me * block, 16), block)
    rows[own_rows, :] = buffer[own_rows, :]
    lax.fori_loop(1, experts, dispatch, 0)

    def stat_plane(j, carry):
        _, device = plane_peer(j)
        pltpu.make_async_remote_copy(
            src_ref=stat, dst_ref=stat_rx.at[me], send_sem=stat_send.at[0],
            recv_sem=stat_recv.at[0], device_id=device, device_id_type=MESH).start()
        return carry

    def stat_dp(j, carry):
        _, device = dp_peer(j)
        pltpu.make_async_remote_copy(
            src_ref=stat_sum, dst_ref=stat_rx2.at[mine], send_sem=stat_send.at[1],
            recv_sem=stat_recv.at[1], device_id=device, device_id_type=MESH).start()
        return carry

    stat_rx[me] = stat[...]
    lax.fori_loop(1, experts, stat_plane, 0)

    def take(ref, sem):
        pltpu.make_async_copy(ref, ref, sem).wait()

    others = (experts - 1) * block

    def first_product(n):
        tile = 256

        def body(t, carry):
            at = pl.ds(pl.multiple_of(t * tile, tile), tile)
            acc = jnp.dot(rows[...], win[n, :, at], preferred_element_type=jnp.float32)
            to = pl.ds(pl.multiple_of(n * cols_in + t * tile, tile), tile)
            hidden[:, to] = gelu(acc).astype(jnp.bfloat16)
            return carry

        lax.fori_loop(0, cols_in // tile, body, 0)

    def send_back(n):
        def body(j, carry):
            p, device = plane_peer(j)
            pltpu.make_async_remote_copy(
                src_ref=served.at[n, pl.ds(pl.multiple_of(p * block, 16), block)],
                dst_ref=returned.at[n, pl.ds(pl.multiple_of(me * block, 16), block)],
                send_sem=back_send.at[n], recv_sem=back_recv.at[n],
                device_id=device, device_id_type=MESH).start()
            return carry

        lax.fori_loop(1, experts, body, 0)

    def combine(n):
        take(returned.at[n, pl.ds(0, others)], back_recv.at[n])
        combined = jnp.dot(placer[...], returned[n], preferred_element_type=jnp.float32)
        mixed_ref[:, n * cols_out:(n + 1) * cols_out] = (
            combined * gate[:, 0:1]).astype(jnp.bfloat16)

    def second_product(n):
        acc = jnp.dot(hidden[...], wout[n], preferred_element_type=jnp.float32)
        served[n] = acc.astype(jnp.bfloat16)
        returned[n, own_rows, :] = served[n, own_rows, :]
        if n > 0:
            combine(n - 1)
        send_back(n)

    last = NZ // 2
    for r in range(chunks + last):
        if 0 < r < chunks:
            send_own(r)
        for hop in range(1, last + 1):
            n = r - hop
            if not 0 <= n < chunks:
                continue
            for direction in range(2):
                ring_arrival(n, direction, hop).wait_recv()
                if hop < last - 1 or hop == last - 1:
                    ring_copy(n, direction, hop + 1).start()
                if hop < last:
                    pair_copy(n, direction, hop, c).start()
            if hop == last:
                pair_copy(n, 0, hop, c).start()
        if r == 1:
            take(rows.at[pl.ds(0, others)], disp_recv)
        if r == 2:
            take(stat_rx.at[pl.ds(0, experts - 1)], stat_recv.at[0])
            total = stat_rx[0]
            for p in range(1, experts):
                total = total + stat_rx[p]
            stat_sum[...] = total
            stat_rx2[mine] = total
        if r == 3:
            lax.fori_loop(1, dps, stat_dp, 0)
        if r == 5:
            take(stat_rx2.at[pl.ds(0, dps - 1)], stat_recv.at[1])
            total = stat_rx2[0]
            for p in range(1, dps):
                total = total + stat_rx2[p]
            modal_counts = total[4:6, 0:experts]
            load_ref[0:2, :] = experts * total[0:2, 0:experts] / modal_counts
            load_ref[2:4, :] = experts * total[2:4, 0:experts] / modal_counts
        n = r - last
        if n >= 0:
            for (direction, hop) in pair_slots():
                pair_copy(n, direction, hop, other).wait_recv()
            if n < CHUNKS_IN:
                first_product(n)
            else:
                second_product(n - CHUNKS_IN)

    for n in range(chunks):
        for direction in range(2):
            for hop in range(1, last + 1):
                ring_copy(n, direction, hop).wait_send()
        for (direction, hop) in pair_slots():
            pair_copy(n, direction, hop, c).wait_send()
    take(buffer.at[pl.ds(0, others)], disp_send)
    take(stat_rx.at[pl.ds(0, experts - 1)], stat_send.at[0])
    take(stat_rx2.at[pl.ds(0, dps - 1)], stat_send.at[1])
    for n in range(CHUNKS_OUT):
        take(served.at[n, pl.ds(0, others)], back_send.at[n])
    combine(CHUNKS_OUT - 1)


def on_device(tokens, modality, routes, router, w_in, w_out):
    micro_count, tok_count, model_width = tokens.shape
    experts = router.shape[1]
    capacity = 2 * tok_count // experts
    toks = micro_count * tok_count
    block = micro_count * capacity
    slots = experts * block
    ff = w_in.shape[2]
    cols_in, cols_out = ff // CHUNKS_IN, model_width // CHUNKS_OUT
    chunks = CHUNKS_IN + CHUNKS_OUT
    half = NZ // 2
    bf16, f32 = jnp.bfloat16, jnp.float32
    vmem = pl.BlockSpec(memory_space=pltpu.VMEM)
    hbm = pl.BlockSpec(memory_space=pltpu.HBM)
    dma = pltpu.SemaphoreType.DMA
    mixed, load = pl.pallas_call(
        layer_kernel,
        out_shape=(
            jax.ShapeDtypeStruct((toks, model_width), bf16),
            jax.ShapeDtypeStruct((4, experts), f32),
        ),
        in_specs=[vmem, vmem, vmem, vmem, hbm, hbm],
        out_specs=(vmem, vmem),
        scratch_shapes=[
            pltpu.VMEM((CHUNKS_IN, model_width, cols_in), bf16),
            pltpu.VMEM((CHUNKS_OUT, ff, cols_out), bf16),
            pltpu.VMEM((toks, slots), bf16),
            pltpu.VMEM((toks, 128), f32),
            pltpu.VMEM((slots, model_width), bf16),
            pltpu.VMEM((slots, model_width), bf16),
            pltpu.VMEM((slots, ff), bf16),
            pltpu.VMEM((CHUNKS_OUT, slots, cols_out), bf16),
            pltpu.VMEM((CHUNKS_OUT, slots, cols_out), bf16),
            pltpu.VMEM((8, 128), f32),
            pltpu.VMEM((experts, 8, 128), f32),
            pltpu.VMEM((8, 128), f32),
            pltpu.VMEM((NZ * NC, 8, 128), f32),
            dma((chunks,)),
            dma((chunks, 2, half)),
            dma((chunks, 2, half)),
            dma((chunks, NZ)),
            dma((chunks, NZ)),
            dma,
            dma,
            dma((CHUNKS_OUT,)),
            dma((CHUNKS_OUT,)),
            dma((2,)),
            dma((2,)),
        ],
        compiler_params=pltpu.CompilerParams(
            collective_id=0, has_side_effects=True, vmem_limit_bytes=60 * 1024 * 1024
        ),
        name="layer",
    )(
        tokens.reshape(toks, model_width),
        routes.reshape(toks, 1),
        modality.reshape(toks, 1),
        router,
        w_in,
        w_out,
    )
    return mixed.reshape(tokens.shape), load.reshape(2, 2, experts)


def solution(mesh):
    torus = Mesh(mesh.devices.reshape(NX, NY, NZ, NC), AXES)
    expert, dp, both = AXES[:2], AXES[2:], AXES
    in_specs = (
        P(None, both, None), P(None, both), P(None, both, None), P(),
        P(expert, dp, None), P(expert, dp, None),
    )
    out_specs = (P(None, both, None), P())
    return jax.shard_map(
        on_device, mesh=torus, in_specs=in_specs, out_specs=out_specs, check_vma=False
    )
```

time: 259 us -> 175 us (0.68)
  Pallas kernels: 0 us -> 169 us
  waiting for transfers between devices: 134 us -> 0 us
  blocking collectives: 74.7 us -> 0 us
  matrix products: 24.7 us -> 0 us
  between operations: 14.2 us -> 0.66 us
  starting transfers between devices: 6.6 us -> 0 us
  local copies, waits for them, and re-layouts: 1.69 us -> 5.72 us
    pallas_call x0 -> x1, Pallas kernels: none -> 169 us  [on_device(): pl.pallas_call(layer_kernel, out_shape=(jax.ShapeDtypeStruct((toks, model...]
    all_gather x2 -> x0, waiting for transfers between devices: 133 us -> none  [the longest x1 78.5 us: on_device(): lax.all_gather(w_in, DP, axis=1, tiled=True)[0]]
    psum x4 -> x0, blocking collectives: 48.4 us -> none  [over_axes(): shard = lax.psum(shard, axis)]
    all_to_all x1 -> x0, blocking collectives: 26.3 us -> none  [on_device(): lax.all_to_all(buffer, EXPERT, split_axis=1, concat_axis=1, tiled=True)]
    dot_general x6 -> x0, matrix products: 24.7 us -> none  [the longest x1 22.4 us: on_device(): jnp.dot(columns, lax.all_gather(w_out, DP, axis=1, tiled=True)[0], prefer...]
    all_to_all x1 -> x0, starting transfers between devices: 6.52 us -> none  [on_device(): lax.all_to_all(served, EXPERT, split_axis=1, concat_axis=1, tiled=True)]
    unnamed x8 -> x11, local copies, waits for them, and re-layouts: 0.03 us -> 4.13 us
  transfers between devices with their start and end apart: 3 -> 0, of which waited for: 2 -> 0; matrix products, arithmetic and copies ran while one was open for 2% -> 0% of each run, Pallas kernels for 0% -> 0%
where the time goes in v1:
time: 175 us
  Pallas kernels  169 us (97%)
  local copies, waits for them, and re-layouts  5.72 us (3%)
    pallas_call x1, Pallas kernels, on_device(): pl.pallas_call(layer_kernel, out_shape=(jax.ShapeDtypeStruct((toks, model...  169 us
    unnamed x11, local copies, waits for them, and re-layouts  4.13 us

profile of v1, /device:TPU:1, one launch (start us, length us, event | category | flops | bytes accessed | tf_op | source)
XLA Modules:
  0.0 175.1 jit_solution(12206299093084557951)
XLA Ops:
  0.6 0.0 copy-start.2
  0.6 0.7 copy-done.2
  1.3 0.0 copy-start.3
  1.3 0.8 copy.10.modality_ref
  2.1 0.0 copy-done.3
  2.1 0.0 copy-start
  2.1 0.8 copy.9.routes_ref
  2.9 0.0 copy-done
  2.9 0.9 copy.11.router_ref
  3.8 168.7 %layer.1 = (bf16[256,1280]{1,0:T(8,128)(2,1)}, f32[4,16]{1,0:T(4,128)}) custom-call(bf16[256,1280]{1,0:T(8,128)(2,1)} %bitcast.6, s32[256,1]{1,0:T(8,128)} %copy.9.routes_ref, s32[256,1]{1,0:T(8,128)} %copy.10.modality_ref, bf16[1280,16]{1,0:T(8,128)(2,1)} %copy.11.router_ref, bf16[1,80,5120]{2,1,0:T(8,128)(2,1)} %w_in_ref.1, bf16[1,320,1280]{2,1,0:T(8,128)(2,1)} %w_out_ref.1), custom_call_target="tpu_custom_call" | custom-call | tf_op jit(solution)/shard_map/layer/pallas_call | solution.py:324
  172.6 0.0 copy-start.1
  172.6 2.0 %copy.14 = bf16[2,128,1280]{2,1,0:T(8,128)(2,1)} copy(bf16[2,128,1280]{2,1,0:T(8,128)(2,1)} %bitcast.5) | data formatting | bytes 1310720
  174.5 0.0 copy-done.1
  174.5 0.6 copy.15
Async XLA Ops:
  0.6 0.7 copy-start.2
  1.3 0.8 copy-start.3
  2.1 0.8 copy-start
  172.6 2.0 %copy-start.1 = (f32[4,16]{1,0:T(4,128)S(1)}, f32[4,16]{1,0:T(4,128)}, u32[]{:S(2)}) copy-start(f32[4,16]{1,0:T(4,128)} %get-tuple-element.5) | copy-start | bytes 772

commit v2 on v1

--- a/solution.py
+++ b/solution.py
@@ -13,7 +13,9 @@
 AXES = ("expert_0", "expert_1", "dp_0", "dp_1")
 MESH = pl.DeviceIdType.MESH
 CHUNKS_IN = 4
-CHUNKS_OUT = 5
+WIDTHS_OUT = (512, 384, 256, 128)
+CHUNKS_OUT = len(WIDTHS_OUT)
+VMEM_BYTES = 65900000
 GELU_C = math.sqrt(2.0 / math.pi)
 
 
@@ -24,19 +26,18 @@
 def layer_kernel(
     tokens_ref, routes_ref, modality_ref, router_ref, w_in_ref, w_out_ref,
     mixed_ref, load_ref,
-    win, wout, placer, gate, buffer, rows, hidden, served, returned,
+    win, wout, tok_buf, placer, gate, buffer, rows, hidden, partial, served, returned,
     stat, stat_rx, stat_sum, stat_rx2,
-    local_sem, ring_send, ring_recv, pair_send, pair_recv,
+    tok_sem, local_sem, ring_send, ring_recv, pair_send, pair_recv,
     disp_send, disp_recv, back_send, back_recv, stat_send, stat_recv,
 ):
     shard_in = w_in_ref.shape[1]
     shard_out = w_out_ref.shape[1]
     width = tokens_ref.shape[1]
     toks = tokens_ref.shape[0]
-    experts = router_ref.shape[1]
+    experts = router_ref.shape[0]
     block = rows.shape[0] // experts
     cols_in = win.shape[2]
-    cols_out = wout.shape[2]
     chunks = CHUNKS_IN + CHUNKS_OUT
     dps = NZ * NC
 
@@ -65,17 +66,19 @@
                     pl.ds(half * (cols_in // 2), cols_in // 2)]
             return view
         if half is None:
-            return wout.at[n - CHUNKS_IN, pl.ds(pl.multiple_of(shard * shard_out, 16), shard_out)]
+            return wout[n - CHUNKS_IN].at[pl.ds(pl.multiple_of(shard * shard_out, 16), shard_out)]
         rows_half = shard_out // 2
-        return wout.at[
-            n - CHUNKS_IN,
+        return wout[n - CHUNKS_IN].at[
             pl.ds(pl.multiple_of(shard * shard_out + half * rows_half, 16), rows_half)]
+
+    def columns(n):
+        return pl.ds(sum(WIDTHS_OUT[:n]), WIDTHS_OUT[n])
 
     def local_copy(n):
         if n < CHUNKS_IN:
             source = w_in_ref.at[0, :, pl.ds(n * cols_in, cols_in)]
         else:
-            source = w_out_ref.at[0, :, pl.ds((n - CHUNKS_IN) * cols_out, cols_out)]
+            source = w_out_ref.at[0, :, columns(n - CHUNKS_IN)]
         return pltpu.make_async_copy(source, piece(n, z, c), local_sem.at[n])
 
     def source_of(direction, hop):
@@ -115,7 +118,10 @@
             send_sem=pair_send.at[n, k], recv_sem=pair_recv.at[n, k],
             device_id=(ex, ey, z, other), device_id_type=MESH)
 
-    for n in range(chunks):
+    local_copy(0).start()
+    tok_copy = pltpu.make_async_copy(tokens_ref, tok_buf, tok_sem)
+    tok_copy.start()
+    for n in range(1, chunks):
         local_copy(n).start()
 
     barrier = pltpu.get_barrier_semaphore()
@@ -141,39 +147,45 @@
         pair_copy(n, 0, 0, c).start()
 
     send_own(0)
-
-    tok = tokens_ref[...]
-    logits = jnp.dot(tok, router_ref[...], preferred_element_type=jnp.float32)
-    lane = lax.broadcasted_iota(jnp.int32, (toks, experts), 1)
-    onehot = (routes_ref[...] == lane).astype(jnp.float32)
-    chosen = jnp.sum(logits * onehot, axis=1, keepdims=True)
-    gate[...] = jnp.broadcast_to(1.0 / (1.0 + jnp.exp(-chosen)), gate.shape)
-    micro_rows = toks // 2
+    send_own(1)
+
+    tok_copy.wait()
+    tok = tok_buf[...]
+    logits = lax.dot_general(
+        router_ref[...], tok, (((1,), (1,)), ((), ())), preferred_element_type=jnp.float32)
+    micro = toks // 2
+    route = jnp.concatenate([routes_ref[0], routes_ref[1]], axis=1)
+    modality = jnp.concatenate([modality_ref[0:1, :], modality_ref[1:2, :]], axis=1)
+    expert_id = lax.broadcasted_iota(jnp.int32, (experts, toks), 0)
+    onehot = (route == expert_id).astype(jnp.float32)
+    chosen = jnp.sum(logits * onehot, axis=0, keepdims=True)
+    gating = 1.0 / (1.0 + jnp.exp(-chosen))
+    for m in range(2):
+        spread = jnp.broadcast_to(gating[:, m * micro:(m + 1) * micro], (micro, micro))
+        gate[m * micro:(m + 1) * micro, :] = spread.T
     row_i = lax.broadcasted_iota(jnp.int32, (toks, toks), 0)
     col_i = lax.broadcasted_iota(jnp.int32, (toks, toks), 1)
-    first = jnp.where(row_i >= micro_rows, micro_rows, 0)
-    earlier = ((col_i <= row_i) & (col_i >= first)).astype(jnp.bfloat16)
-    running = jnp.dot(earlier, onehot.astype(jnp.bfloat16), preferred_element_type=jnp.float32)
-    lane_f = lane.astype(jnp.float32)
-    spot = jnp.sum((running - 1.0 + lane_f * block) * onehot, axis=1, keepdims=True)
-    token_id = lax.broadcasted_iota(jnp.int32, (toks, 1), 0)
-    spot = spot + jnp.where(token_id >= micro_rows, block // 2, 0).astype(jnp.float32)
-    slots = lax.broadcasted_iota(jnp.int32, (toks, experts * block), 1).astype(jnp.float32)
+    first = jnp.where(col_i >= micro, micro, 0)
+    earlier = ((row_i <= col_i) & (row_i >= first)).astype(jnp.bfloat16)
+    running = jnp.dot(onehot.astype(jnp.bfloat16), earlier, preferred_element_type=jnp.float32)
+    spot = jnp.sum(
+        (running - 1.0 + expert_id.astype(jnp.float32) * block) * onehot, axis=0, keepdims=True)
+    token_id = lax.broadcasted_iota(jnp.int32, (1, toks), 1)
+    spot = spot + jnp.where(token_id >= micro, block // 2, 0).astype(jnp.float32)
+    slots = lax.broadcasted_iota(jnp.int32, (experts * block, toks), 0).astype(jnp.float32)
     place = (spot == slots).astype(jnp.bfloat16)
     placer[...] = place
-    buffer[...] = lax.dot_general(
-        place, tok, (((0,), (0,)), ((), ())), preferred_element_type=jnp.float32
-    ).astype(jnp.bfloat16)
+    buffer[...] = jnp.dot(place, tok, preferred_element_type=jnp.float32).astype(jnp.bfloat16)
 
     exps = jnp.exp(logits)
-    probs = exps / jnp.sum(exps, axis=1, keepdims=True)
+    probs = exps / jnp.sum(exps, axis=0, keepdims=True)
     stat[...] = jnp.zeros(stat.shape, jnp.float32)
     for k in range(2):
-        modal = (modality_ref[...] == k).astype(jnp.float32)
-        stat[k:k + 1, 0:experts] = jnp.sum(onehot * modal, axis=0, keepdims=True)
-        stat[2 + k:3 + k, 0:experts] = jnp.sum(probs * modal, axis=0, keepdims=True)
-        stat[4 + k:5 + k, 0:experts] = jnp.sum(
-            jnp.broadcast_to(modal, (toks, experts)), axis=0, keepdims=True)
+        modal = (modality == k).astype(jnp.float32)
+        stat[:, k:k + 1] = jnp.sum(onehot * modal, axis=1, keepdims=True)
+        stat[:, 2 + k:3 + k] = jnp.sum(probs * modal, axis=1, keepdims=True)
+        stat[:, 4 + k:5 + k] = jnp.sum(
+            jnp.broadcast_to(modal, (experts, toks)), axis=1, keepdims=True)
 
     def dispatch(j, carry):
         p, device = plane_peer(j)
@@ -226,8 +238,8 @@
         def body(j, carry):
             p, device = plane_peer(j)
             pltpu.make_async_remote_copy(
-                src_ref=served.at[n, pl.ds(pl.multiple_of(p * block, 16), block)],
-                dst_ref=returned.at[n, pl.ds(pl.multiple_of(me * block, 16), block)],
+                src_ref=served[n].at[pl.ds(pl.multiple_of(p * block, 16), block)],
+                dst_ref=returned[n].at[pl.ds(pl.multiple_of(me * block, 16), block)],
                 send_sem=back_send.at[n], recv_sem=back_recv.at[n],
                 device_id=device, device_id_type=MESH).start()
             return carry
@@ -235,37 +247,49 @@
         lax.fori_loop(1, experts, body, 0)
 
     def combine(n):
-        take(returned.at[n, pl.ds(0, others)], back_recv.at[n])
-        combined = jnp.dot(placer[...], returned[n], preferred_element_type=jnp.float32)
-        mixed_ref[:, n * cols_out:(n + 1) * cols_out] = (
-            combined * gate[:, 0:1]).astype(jnp.bfloat16)
-
-    def second_product(n):
-        acc = jnp.dot(hidden[...], wout[n], preferred_element_type=jnp.float32)
-        served[n] = acc.astype(jnp.bfloat16)
-        returned[n, own_rows, :] = served[n, own_rows, :]
-        if n > 0:
-            combine(n - 1)
+        take(returned[n].at[pl.ds(0, others)], back_recv.at[n])
+        combined = lax.dot_general(
+            placer[...], returned[n][...], (((0,), (0,)), ((), ())),
+            preferred_element_type=jnp.float32)
+        mixed_ref[:, columns(n)] = (combined * gate[:, 0:1]).astype(jnp.bfloat16)
+
+    chip_out = NC * shard_out
+
+    def term(n, source_z):
+        at = pl.ds(pl.multiple_of(source_z * chip_out, 128), chip_out)
+        return jnp.dot(hidden[:, at], wout[n][at, :], preferred_element_type=jnp.float32)
+
+    def second_product_start(n):
+        width = pl.ds(0, WIDTHS_OUT[n])
+        partial[:, width] = term(n, z)
+
+        def body(k, carry):
+            partial[:, width] += term(n, lax.rem(z + NZ // 2 + k, NZ))
+            return carry
+
+        lax.fori_loop(1, NZ // 2, body, 0)
+        lax.fori_loop(NZ // 2 + 1, NZ, body, 0)
+
+    def second_product_end(n):
+        acc = partial[:, pl.ds(0, WIDTHS_OUT[n])] + term(n, lax.rem(z + NZ // 2, NZ))
+        served[n][...] = acc.astype(jnp.bfloat16)
+        returned[n][own_rows, :] = served[n][own_rows, :]
         send_back(n)
+        if n > 1:
+            combine(n - 2)
 
     last = NZ // 2
-    for r in range(chunks + last):
-        if 0 < r < chunks:
-            send_own(r)
-        for hop in range(1, last + 1):
+    for r in range(1, chunks + last):
+        if r < chunks - 1:
+            send_own(r + 1)
+        for hop in range(1, last):
             n = r - hop
             if not 0 <= n < chunks:
                 continue
             for direction in range(2):
                 ring_arrival(n, direction, hop).wait_recv()
-                if hop < last - 1 or hop == last - 1:
-                    ring_copy(n, direction, hop + 1).start()
-                if hop < last:
-                    pair_copy(n, direction, hop, c).start()
-            if hop == last:
-                pair_copy(n, 0, hop, c).start()
-        if r == 1:
-            take(rows.at[pl.ds(0, others)], disp_recv)
+                ring_copy(n, direction, hop + 1).start()
+                pair_copy(n, direction, hop, c).start()
         if r == 2:
             take(stat_rx.at[pl.ds(0, experts - 1)], stat_recv.at[0])
             total = stat_rx[0]
@@ -280,17 +304,31 @@
             total = stat_rx2[0]
             for p in range(1, dps):
                 total = total + stat_rx2[p]
-            modal_counts = total[4:6, 0:experts]
-            load_ref[0:2, :] = experts * total[0:2, 0:experts] / modal_counts
-            load_ref[2:4, :] = experts * total[2:4, 0:experts] / modal_counts
+            flat = total.T
+            modal_counts = flat[4:6, 0:experts]
+            load_ref[0] = experts * flat[0:2, 0:experts] / modal_counts
+            load_ref[1] = experts * flat[2:4, 0:experts] / modal_counts
         n = r - last
-        if n >= 0:
-            for (direction, hop) in pair_slots():
-                pair_copy(n, direction, hop, other).wait_recv()
-            if n < CHUNKS_IN:
-                first_product(n)
-            else:
-                second_product(n - CHUNKS_IN)
+        if n < 0:
+            continue
+        slots_now = pair_slots()
+        for (direction, hop) in slots_now[:-1]:
+            pair_copy(n, direction, hop, other).wait_recv()
+        if n >= CHUNKS_IN:
+            second_product_start(n - CHUNKS_IN)
+        for direction in range(2):
+            ring_arrival(n, direction, last).wait_recv()
+        pair_copy(n, 0, last, c).start()
+        if n == 0:
+            take(rows.at[pl.ds(0, others)], disp_recv)
+        pair_copy(n, 0, last, other).wait_recv()
+        if n < CHUNKS_IN:
+            first_product(n)
+        else:
+            second_product_end(n - CHUNKS_IN)
+
+    combine(CHUNKS_OUT - 2)
+    combine(CHUNKS_OUT - 1)
 
     for n in range(chunks):
         for direction in range(2):
@@ -302,8 +340,7 @@
     take(stat_rx.at[pl.ds(0, experts - 1)], stat_send.at[0])
     take(stat_rx2.at[pl.ds(0, dps - 1)], stat_send.at[1])
     for n in range(CHUNKS_OUT):
-        take(served.at[n, pl.ds(0, others)], back_send.at[n])
-    combine(CHUNKS_OUT - 1)
+        take(served[n].at[pl.ds(0, others)], back_send.at[n])
 
 
 def on_device(tokens, modality, routes, router, w_in, w_out):
@@ -314,7 +351,7 @@
     block = micro_count * capacity
     slots = experts * block
     ff = w_in.shape[2]
-    cols_in, cols_out = ff // CHUNKS_IN, model_width // CHUNKS_OUT
+    cols_in = ff // CHUNKS_IN
     chunks = CHUNKS_IN + CHUNKS_OUT
     half = NZ // 2
     bf16, f32 = jnp.bfloat16, jnp.float32
@@ -325,24 +362,27 @@
         layer_kernel,
         out_shape=(
             jax.ShapeDtypeStruct((toks, model_width), bf16),
-            jax.ShapeDtypeStruct((4, experts), f32),
+            jax.ShapeDtypeStruct((2, 2, experts), f32),
         ),
-        in_specs=[vmem, vmem, vmem, vmem, hbm, hbm],
+        in_specs=[hbm, vmem, vmem, vmem, hbm, hbm],
         out_specs=(vmem, vmem),
         scratch_shapes=[
             pltpu.VMEM((CHUNKS_IN, model_width, cols_in), bf16),
-            pltpu.VMEM((CHUNKS_OUT, ff, cols_out), bf16),
-            pltpu.VMEM((toks, slots), bf16),
+            [pltpu.VMEM((ff, w), bf16) for w in WIDTHS_OUT],
+            pltpu.VMEM((toks, model_width), bf16),
+            pltpu.VMEM((slots, toks), bf16),
             pltpu.VMEM((toks, 128), f32),
             pltpu.VMEM((slots, model_width), bf16),
             pltpu.VMEM((slots, model_width), bf16),
             pltpu.VMEM((slots, ff), bf16),
-            pltpu.VMEM((CHUNKS_OUT, slots, cols_out), bf16),
-            pltpu.VMEM((CHUNKS_OUT, slots, cols_out), bf16),
-            pltpu.VMEM((8, 128), f32),
-            pltpu.VMEM((experts, 8, 128), f32),
-            pltpu.VMEM((8, 128), f32),
-            pltpu.VMEM((NZ * NC, 8, 128), f32),
+            pltpu.VMEM((slots, max(WIDTHS_OUT)), f32),
+            [pltpu.VMEM((slots, w), bf16) for w in WIDTHS_OUT],
+            [pltpu.VMEM((slots, w), bf16) for w in WIDTHS_OUT],
+            pltpu.VMEM((experts, 128), f32),
+            pltpu.VMEM((experts, experts, 128), f32),
+            pltpu.VMEM((experts, 128), f32),
+            pltpu.VMEM((NZ * NC, experts, 128), f32),
+            dma,
             dma((chunks,)),
             dma((chunks, 2, half)),
             dma((chunks, 2, half)),
@@ -356,18 +396,18 @@
             dma((2,)),
         ],
         compiler_params=pltpu.CompilerParams(
-            collective_id=0, has_side_effects=True, vmem_limit_bytes=60 * 1024 * 1024
+            collective_id=0, has_side_effects=True, vmem_limit_bytes=VMEM_BYTES
         ),
         name="layer",
     )(
         tokens.reshape(toks, model_width),
-        routes.reshape(toks, 1),
-        modality.reshape(toks, 1),
-        router,
+        jnp.transpose(routes, (0, 2, 1)),
+        modality,
+        router.T,
         w_in,
         w_out,
     )
-    return mixed.reshape(tokens.shape), load.reshape(2, 2, experts)
+    return mixed.reshape(tokens.shape), load
 
 
 def solution(mesh):

time: 175 us -> 160 us (0.914)
  Pallas kernels: 169 us -> 157 us
  local copies, waits for them, and re-layouts: 5.72 us -> 2.55 us
    pallas_call x1, Pallas kernels: 169 us -> 157 us  [on_device(): pl.pallas_call(layer_kernel, out_shape=(jax.ShapeDtypeStruct((toks, model...]
    unnamed x11 -> x4, local copies, waits for them, and re-layouts: 4.13 us -> 2.55 us
where the time goes in v2:
time: 160 us
  Pallas kernels  157 us (98%)
  local copies, waits for them, and re-layouts  2.55 us (2%)
    pallas_call x1, Pallas kernels, on_device(): pl.pallas_call(layer_kernel, out_shape=(jax.ShapeDtypeStruct((toks, model...  157 us

profile of v2, /device:TPU:1, one launch (start us, length us, event | category | flops | bytes accessed | tf_op | source)
XLA Modules:
  0.0 160.0 jit_solution(7184196493424404983)
XLA Ops:
  0.6 156.9 %layer.1 = (bf16[256,1280]{1,0:T(8,128)(2,1)}, f32[2,2,16]{2,1,0:T(2,128)}) custom-call(bf16[256,1280]{1,0:T(8,128)(2,1)} %bitcast.5, s32[2,1,128]{2,1,0:T(1,128)} %bitcast.7, s32[2,128]{1,0:T(2,128)} %modality_ref.1, bf16[16,1280]{1,0:T(8,128)(2,1)} %bitcast.6, bf16[1,80,5120]{2,1,0:T(8,128)(2,1)} %w_in_ref.1, bf16[1,320,1280]{2,1,0:T(8,128)(2,1)} %w_out_ref.1), custom_call_target="tpu_custom_call" | custom-call | tf_op jit(solution)/shard_map/layer/pallas_call | solution.py:361
  157.5 0.0 copy-start
  157.5 2.0 %copy.10 = bf16[2,128,1280]{2,1,0:T(8,128)(2,1)} copy(bf16[2,128,1280]{2,1,0:T(8,128)(2,1)} %bitcast.4) | data formatting | bytes 1310720
  159.5 0.0 copy-done
  159.5 0.6 copy.11
Async XLA Ops:
  157.5 2.0 %copy-start = (f32[2,2,16]{2,1,0:T(2,128)S(1)}, f32[2,2,16]{2,1,0:T(2,128)}, u32[]{:S(2)}) copy-start(f32[2,2,16]{2,1,0:T(2,128)} %get-tuple-element.9) | copy-start | bytes 772

commit v3 on v2

--- a/solution.py
+++ b/solution.py
@@ -26,10 +26,10 @@
 def layer_kernel(
     tokens_ref, routes_ref, modality_ref, router_ref, w_in_ref, w_out_ref,
     mixed_ref, load_ref,
-    win, wout, tok_buf, placer, gate, buffer, rows, hidden, partial, served, returned,
+    win, wout, tok_buf, placer, gate, buffer, rows, hidden, served, returned,
     stat, stat_rx, stat_sum, stat_rx2,
     tok_sem, local_sem, ring_send, ring_recv, pair_send, pair_recv,
-    disp_send, disp_recv, back_send, back_recv, stat_send, stat_recv,
+    disp_send, disp_recv, back_send, back_recv, stat_send, stat_recv, row_in,
 ):
     shard_in = w_in_ref.shape[1]
     shard_out = w_out_ref.shape[1]
@@ -126,19 +126,16 @@
 
     barrier = pltpu.get_barrier_semaphore()
 
-    def greet_plane(j, carry):
-        _, device = plane_peer(j)
-        pl.semaphore_signal(barrier, inc=1, device_id=device, device_id_type=MESH)
-        return carry
-
-    def greet_dp(j, carry):
-        _, device = dp_peer(j)
-        pl.semaphore_signal(barrier, inc=1, device_id=device, device_id_type=MESH)
-        return carry
-
-    lax.fori_loop(1, dps, greet_dp, 0)
-    lax.fori_loop(1, experts, greet_plane, 0)
-    pl.semaphore_wait(barrier, experts + dps - 2)
+    x_sides = [(lax.rem(ex + d, NX), ey, z, c) for d in (1, NX - 1)]
+    y_sides = [(ex, lax.rem(ey + d, NY), z, c) for d in (1, NY - 1)]
+    z_sides = [(ex, ey, up, c), (ex, ey, down, c), (ex, ey, z, other)]
+
+    def signal_all(sem, devices):
+        for device in devices:
+            pl.semaphore_signal(sem, inc=1, device_id=device, device_id_type=MESH)
+
+    signal_all(barrier, z_sides + x_sides + y_sides)
+    pl.semaphore_wait(barrier, len(z_sides + x_sides + y_sides))
 
     def send_own(n):
         local_copy(n).wait()
@@ -148,6 +145,7 @@
 
     send_own(0)
     send_own(1)
+    signal_all(row_in.at[0], x_sides)
 
     tok_copy.wait()
     tok = tok_buf[...]
@@ -174,7 +172,7 @@
     spot = spot + jnp.where(token_id >= micro, block // 2, 0).astype(jnp.float32)
     slots = lax.broadcasted_iota(jnp.int32, (experts * block, toks), 0).astype(jnp.float32)
     place = (spot == slots).astype(jnp.bfloat16)
-    placer[...] = place
+    placer[...] = place.T
     buffer[...] = jnp.dot(place, tok, preferred_element_type=jnp.float32).astype(jnp.bfloat16)
 
     exps = jnp.exp(logits)
@@ -187,6 +185,11 @@
         stat[:, 4 + k:5 + k] = jnp.sum(
             jnp.broadcast_to(modal, (experts, toks)), axis=1, keepdims=True)
 
+    pl.semaphore_wait(row_in.at[0], 2)
+    signal_all(row_in.at[1], y_sides)
+    pl.semaphore_wait(row_in.at[1], 2)
+    signal_all(row_in.at[2], y_sides)
+
     def dispatch(j, carry):
         p, device = plane_peer(j)
         pltpu.make_async_remote_copy(
@@ -198,6 +201,7 @@
 
     own_rows = pl.ds(pl.multiple_of(me * block, 16), block)
     rows[own_rows, :] = buffer[own_rows, :]
+    pl.semaphore_wait(row_in.at[2], 2)
     lax.fori_loop(1, experts, dispatch, 0)
 
     def stat_plane(j, carry):
@@ -234,49 +238,43 @@
 
         lax.fori_loop(0, cols_in // tile, body, 0)
 
+    def apart(d):
+        return min(d[0], NX - d[0]) + min(d[1], NY - d[1])
+
+    steps = [(dx, dy) for dx in range(NX) for dy in range(NY) if (dx, dy) != (0, 0)]
+    steps.sort(key=apart, reverse=True)
+
     def send_back(n):
-        def body(j, carry):
-            p, device = plane_peer(j)
+        for dx, dy in steps:
+            px, py = lax.rem(ex + dx, NX), lax.rem(ey + dy, NY)
+            p, device = px * NY + py, (px, py, z, c)
             pltpu.make_async_remote_copy(
                 src_ref=served[n].at[pl.ds(pl.multiple_of(p * block, 16), block)],
                 dst_ref=returned[n].at[pl.ds(pl.multiple_of(me * block, 16), block)],
                 send_sem=back_send.at[n], recv_sem=back_recv.at[n],
                 device_id=device, device_id_type=MESH).start()
-            return carry
-
-        lax.fori_loop(1, experts, body, 0)
 
     def combine(n):
         take(returned[n].at[pl.ds(0, others)], back_recv.at[n])
-        combined = lax.dot_general(
-            placer[...], returned[n][...], (((0,), (0,)), ((), ())),
-            preferred_element_type=jnp.float32)
+        combined = jnp.dot(
+            placer[...], returned[n][...], preferred_element_type=jnp.float32)
         mixed_ref[:, columns(n)] = (combined * gate[:, 0:1]).astype(jnp.bfloat16)
 
-    chip_out = NC * shard_out
-
-    def term(n, source_z):
-        at = pl.ds(pl.multiple_of(source_z * chip_out, 128), chip_out)
-        return jnp.dot(hidden[:, at], wout[n][at, :], preferred_element_type=jnp.float32)
-
-    def second_product_start(n):
-        width = pl.ds(0, WIDTHS_OUT[n])
-        partial[:, width] = term(n, z)
-
-        def body(k, carry):
-            partial[:, width] += term(n, lax.rem(z + NZ // 2 + k, NZ))
-            return carry
-
-        lax.fori_loop(1, NZ // 2, body, 0)
-        lax.fori_loop(NZ // 2 + 1, NZ, body, 0)
-
-    def second_product_end(n):
-        acc = partial[:, pl.ds(0, WIDTHS_OUT[n])] + term(n, lax.rem(z + NZ // 2, NZ))
+    def second_product(n):
+        acc = jnp.dot(hidden[...], wout[n][...], preferred_element_type=jnp.float32)
         served[n][...] = acc.astype(jnp.bfloat16)
         returned[n][own_rows, :] = served[n][own_rows, :]
         send_back(n)
         if n > 1:
             combine(n - 2)
+
+    def product(n):
+        for (direction, hop) in pair_slots():
+            pair_copy(n, direction, hop, other).wait_recv()
+        if n < CHUNKS_IN:
+            first_product(n)
+        else:
+            second_product(n - CHUNKS_IN)
 
     last = NZ // 2
     for r in range(1, chunks + last):
@@ -290,16 +288,24 @@
                 ring_arrival(n, direction, hop).wait_recv()
                 ring_copy(n, direction, hop + 1).start()
                 pair_copy(n, direction, hop, c).start()
-        if r == 2:
+        n = r - last
+        if n >= 0:
+            for direction in range(2):
+                ring_arrival(n, direction, last).wait_recv()
+            pair_copy(n, 0, last, c).start()
+        if n == 0:
+            take(rows.at[pl.ds(0, others)], disp_recv)
             take(stat_rx.at[pl.ds(0, experts - 1)], stat_recv.at[0])
             total = stat_rx[0]
             for p in range(1, experts):
                 total = total + stat_rx[p]
             stat_sum[...] = total
             stat_rx2[mine] = total
-        if r == 3:
+        if n >= 0:
+            product(n)
+        if n == 1:
             lax.fori_loop(1, dps, stat_dp, 0)
-        if r == 5:
+        if n == 3:
             take(stat_rx2.at[pl.ds(0, dps - 1)], stat_recv.at[1])
             total = stat_rx2[0]
             for p in range(1, dps):
@@ -308,24 +314,6 @@
             modal_counts = flat[4:6, 0:experts]
             load_ref[0] = experts * flat[0:2, 0:experts] / modal_counts
             load_ref[1] = experts * flat[2:4, 0:experts] / modal_counts
-        n = r - last
-        if n < 0:
-            continue
-        slots_now = pair_slots()
-        for (direction, hop) in slots_now[:-1]:
-            pair_copy(n, direction, hop, other).wait_recv()
-        if n >= CHUNKS_IN:
-            second_product_start(n - CHUNKS_IN)
-        for direction in range(2):
-            ring_arrival(n, direction, last).wait_recv()
-        pair_copy(n, 0, last, c).start()
-        if n == 0:
-            take(rows.at[pl.ds(0, others)], disp_recv)
-        pair_copy(n, 0, last, other).wait_recv()
-        if n < CHUNKS_IN:
-            first_product(n)
-        else:
-            second_product_end(n - CHUNKS_IN)
 
     combine(CHUNKS_OUT - 2)
     combine(CHUNKS_OUT - 1)
@@ -361,8 +349,8 @@
     mixed, load = pl.pallas_call(
         layer_kernel,
         out_shape=(
-            jax.ShapeDtypeStruct((toks, model_width), bf16),
-            jax.ShapeDtypeStruct((2, 2, experts), f32),
+            pltpu.VMEM((toks, model_width), bf16),
+            pltpu.VMEM((2, 2, experts), f32),
         ),
         in_specs=[hbm, vmem, vmem, vmem, hbm, hbm],
         out_specs=(vmem, vmem),
@@ -370,12 +358,11 @@
             pltpu.VMEM((CHUNKS_IN, model_width, cols_in), bf16),
             [pltpu.VMEM((ff, w), bf16) for w in WIDTHS_OUT],
             pltpu.VMEM((toks, model_width), bf16),
-            pltpu.VMEM((slots, toks), bf16),
+            pltpu.VMEM((toks, slots), bf16),
             pltpu.VMEM((toks, 128), f32),
             pltpu.VMEM((slots, model_width), bf16),
             pltpu.VMEM((slots, model_width), bf16),
             pltpu.VMEM((slots, ff), bf16),
-            pltpu.VMEM((slots, max(WIDTHS_OUT)), f32),
             [pltpu.VMEM((slots, w), bf16) for w in WIDTHS_OUT],
             [pltpu.VMEM((slots, w), bf16) for w in WIDTHS_OUT],
             pltpu.VMEM((experts, 128), f32),
@@ -394,6 +381,7 @@
             dma((CHUNKS_OUT,)),
             dma((2,)),
             dma((2,)),
+            pltpu.SemaphoreType.REGULAR((3,)),
         ],
         compiler_params=pltpu.CompilerParams(
             collective_id=0, has_side_effects=True, vmem_limit_bytes=VMEM_BYTES

time: 160 us -> 156 us (0.975)
  Pallas kernels: 157 us -> 153 us
    pallas_call x1, Pallas kernels: 157 us -> 153 us  [on_device(): pl.pallas_call(layer_kernel, out_shape=(pltpu.VMEM((toks, model_width), b...]
where the time goes in v3:
time: 156 us; the launch traced here: 155 us
  Pallas kernels  153 us (98%)
    pallas_call x1, Pallas kernels, on_device(): pl.pallas_call(layer_kernel, out_shape=(pltpu.VMEM((toks, model_width), b...  153 us

profile of v3, /device:TPU:1, one launch (start us, length us, event | category | flops | bytes accessed | tf_op | source)
XLA Modules:
  0.0 155.5 jit_solution(9750581348265181092)
XLA Ops:
  0.6 153.4 %layer.1 = (bf16[256,1280]{1,0:T(8,128)(2,1)S(1)}, f32[2,2,16]{2,1,0:T(2,128)S(1)}) custom-call(bf16[256,1280]{1,0:T(8,128)(2,1)} %bitcast.5, s32[2,1,128]{2,1,0:T(1,128)} %bitcast.7, s32[2,128]{1,0:T(2,128)} %modality_ref.1, bf16[16,1280]{1,0:T(8,128)(2,1)} %bitcast.6, bf16[1,80,5120]{2,1,0:T(8,128)(2,1)} %w_in_ref.1, bf16[1,320,1280]{2,1,0:T(8,128)(2,1)} %w_out_ref.1), custom_call_target="tpu_custom_call" | custom-call | tf_op jit(solution)/shard_map/layer/pallas_call | solution.py:349
  154.0 0.8 copy.10
  154.9 0.6 copy.11

commit v4 on v3

--- a/solution.py
+++ b/solution.py
@@ -24,18 +24,18 @@
 
 
 def layer_kernel(
-    tokens_ref, routes_ref, modality_ref, router_ref, w_in_ref, w_out_ref,
+    tokens_ref, routes_hbm, modality_hbm, router_hbm, w_in_ref, w_out_ref,
     mixed_ref, load_ref,
-    win, wout, tok_buf, placer, gate, buffer, rows, hidden, served, returned,
+    routes_ref, modality_ref, router_ref, win, wout, tok_buf, placer, gate, buffer, rows, hidden, served, returned,
     stat, stat_rx, stat_sum, stat_rx2,
     tok_sem, local_sem, ring_send, ring_recv, pair_send, pair_recv,
-    disp_send, disp_recv, back_send, back_recv, stat_send, stat_recv, row_in,
+    disp_send, disp_recv, back_send, back_recv, stat_send, stat_recv, row_in, cross_send, cross_recv,
 ):
     shard_in = w_in_ref.shape[1]
     shard_out = w_out_ref.shape[1]
     width = tokens_ref.shape[1]
     toks = tokens_ref.shape[0]
-    experts = router_ref.shape[0]
+    experts = router_hbm.shape[0]
     block = rows.shape[0] // experts
     cols_in = win.shape[2]
     chunks = CHUNKS_IN + CHUNKS_OUT
@@ -118,12 +118,6 @@
             send_sem=pair_send.at[n, k], recv_sem=pair_recv.at[n, k],
             device_id=(ex, ey, z, other), device_id_type=MESH)
 
-    local_copy(0).start()
-    tok_copy = pltpu.make_async_copy(tokens_ref, tok_buf, tok_sem)
-    tok_copy.start()
-    for n in range(1, chunks):
-        local_copy(n).start()
-
     barrier = pltpu.get_barrier_semaphore()
 
     x_sides = [(lax.rem(ex + d, NX), ey, z, c) for d in (1, NX - 1)]
@@ -135,6 +129,24 @@
             pl.semaphore_signal(sem, inc=1, device_id=device, device_id_type=MESH)
 
     signal_all(barrier, z_sides + x_sides + y_sides)
+    def cross_copy(n, direction, core, hop):
+        ref = piece(n, source_of(direction, hop), core, direction)
+        return pltpu.make_async_remote_copy(
+            src_ref=ref, dst_ref=ref,
+            send_sem=cross_send.at[direction], recv_sem=cross_recv.at[direction],
+            device_id=(ex, ey, up if direction == 0 else down, other), device_id_type=MESH)
+
+    local_copy(0).start()
+    inputs = [(tokens_ref, tok_buf), (routes_hbm, routes_ref), (modality_hbm, modality_ref),
+              (router_hbm, router_ref)]
+    input_copies = [
+        pltpu.make_async_copy(source, target, tok_sem.at[k])
+        for k, (source, target) in enumerate(inputs)]
+    for n in range(1, chunks):
+        local_copy(n).start()
+        if n == 1:
+            for copy in input_copies:
+                copy.start()
     pl.semaphore_wait(barrier, len(z_sides + x_sides + y_sides))
 
     def send_own(n):
@@ -147,7 +159,8 @@
     send_own(1)
     signal_all(row_in.at[0], x_sides)
 
-    tok_copy.wait()
+    for copy in input_copies:
+        copy.wait()
     tok = tok_buf[...]
     logits = lax.dot_general(
         router_ref[...], tok, (((1,), (1,)), ((), ())), preferred_element_type=jnp.float32)
@@ -270,7 +283,11 @@
 
     def product(n):
         for (direction, hop) in pair_slots():
-            pair_copy(n, direction, hop, other).wait_recv()
+            if n < chunks - 1 or hop < last:
+                pair_copy(n, direction, hop, other).wait_recv()
+        if n == chunks - 1:
+            for direction in range(2):
+                cross_copy(n, direction, other, last).wait_recv()
         if n < CHUNKS_IN:
             first_product(n)
         else:
@@ -287,12 +304,15 @@
             for direction in range(2):
                 ring_arrival(n, direction, hop).wait_recv()
                 ring_copy(n, direction, hop + 1).start()
+                if n == chunks - 1 and hop == last - 1:
+                    cross_copy(n, direction, c, hop).start()
                 pair_copy(n, direction, hop, c).start()
         n = r - last
         if n >= 0:
             for direction in range(2):
                 ring_arrival(n, direction, last).wait_recv()
-            pair_copy(n, 0, last, c).start()
+            if n < chunks - 1:
+                pair_copy(n, 0, last, c).start()
         if n == 0:
             take(rows.at[pl.ds(0, others)], disp_recv)
             take(stat_rx.at[pl.ds(0, experts - 1)], stat_recv.at[0])
@@ -315,18 +335,20 @@
             load_ref[0] = experts * flat[0:2, 0:experts] / modal_counts
             load_ref[1] = experts * flat[2:4, 0:experts] / modal_counts
 
-    combine(CHUNKS_OUT - 2)
-    combine(CHUNKS_OUT - 1)
-
     for n in range(chunks):
         for direction in range(2):
             for hop in range(1, last + 1):
                 ring_copy(n, direction, hop).wait_send()
         for (direction, hop) in pair_slots():
-            pair_copy(n, direction, hop, c).wait_send()
+            if n < chunks - 1 or hop < last:
+                pair_copy(n, direction, hop, c).wait_send()
+    for direction in range(2):
+        cross_copy(chunks - 1, direction, c, last - 1).wait_send()
     take(buffer.at[pl.ds(0, others)], disp_send)
     take(stat_rx.at[pl.ds(0, experts - 1)], stat_send.at[0])
     take(stat_rx2.at[pl.ds(0, dps - 1)], stat_send.at[1])
+    combine(CHUNKS_OUT - 2)
+    combine(CHUNKS_OUT - 1)
     for n in range(CHUNKS_OUT):
         take(served[n].at[pl.ds(0, others)], back_send.at[n])
 
@@ -352,9 +374,12 @@
             pltpu.VMEM((toks, model_width), bf16),
             pltpu.VMEM((2, 2, experts), f32),
         ),
-        in_specs=[hbm, vmem, vmem, vmem, hbm, hbm],
+        in_specs=[hbm] * 6,
         out_specs=(vmem, vmem),
         scratch_shapes=[
+            pltpu.VMEM((micro_count, 1, tok_count), jnp.int32),
+            pltpu.VMEM((micro_count, tok_count), jnp.int32),
+            pltpu.VMEM((experts, model_width), bf16),
             pltpu.VMEM((CHUNKS_IN, model_width, cols_in), bf16),
             [pltpu.VMEM((ff, w), bf16) for w in WIDTHS_OUT],
             pltpu.VMEM((toks, model_width), bf16),
@@ -369,7 +394,7 @@
             pltpu.VMEM((experts, experts, 128), f32),
             pltpu.VMEM((experts, 128), f32),
             pltpu.VMEM((NZ * NC, experts, 128), f32),
-            dma,
+            dma((4,)),
             dma((chunks,)),
             dma((chunks, 2, half)),
             dma((chunks, 2, half)),
@@ -382,6 +407,8 @@
             dma((2,)),
             dma((2,)),
             pltpu.SemaphoreType.REGULAR((3,)),
+            dma((2,)),
+            dma((2,)),
         ],
         compiler_params=pltpu.CompilerParams(
             collective_id=0, has_side_effects=True, vmem_limit_bytes=VMEM_BYTES

time: 156 us -> 153 us (0.981)
  Pallas kernels: 153 us -> 150 us
    pallas_call x1, Pallas kernels: 153 us -> 150 us  [on_device(): pl.pallas_call(layer_kernel, out_shape=(pltpu.VMEM((toks, model_width), b...]
where the time goes in v4:
time: 153 us; the launch traced here: 152 us
  Pallas kernels  150 us (98%)
    pallas_call x1, Pallas kernels, on_device(): pl.pallas_call(layer_kernel, out_shape=(pltpu.VMEM((toks, model_width), b...  150 us

profile of v4, /device:TPU:1, one launch (start us, length us, event | category | flops | bytes accessed | tf_op | source)
XLA Modules:
  0.0 152.3 jit_solution(12628398935398573703)
XLA Ops:
  0.6 150.2 %layer.1 = (bf16[256,1280]{1,0:T(8,128)(2,1)S(1)}, f32[2,2,16]{2,1,0:T(2,128)S(1)}) custom-call(bf16[256,1280]{1,0:T(8,128)(2,1)} %bitcast.5, s32[2,1,128]{2,1,0:T(1,128)} %bitcast.7, s32[2,128]{1,0:T(2,128)} %modality_hbm.1, bf16[16,1280]{1,0:T(8,128)(2,1)} %bitcast.6, bf16[1,80,5120]{2,1,0:T(8,128)(2,1)} %w_in_ref.1, bf16[1,320,1280]{2,1,0:T(8,128)(2,1)} %w_out_ref.1), custom_call_target="tpu_custom_call" | custom-call | tf_op jit(solution)/shard_map/layer/pallas_call | solution.py:371
  150.9 0.8 copy.10
  151.7 0.6 copy.11

commit v5 on v4

--- a/solution.py
+++ b/solution.py
@@ -12,7 +12,7 @@
 NX, NY, NZ, NC = 4, 4, 8, 2
 AXES = ("expert_0", "expert_1", "dp_0", "dp_1")
 MESH = pl.DeviceIdType.MESH
-CHUNKS_IN = 4
+CHUNKS_IN = 2
 WIDTHS_OUT = (512, 384, 256, 128)
 CHUNKS_OUT = len(WIDTHS_OUT)
 VMEM_BYTES = 65900000
@@ -26,7 +26,7 @@
 def layer_kernel(
     tokens_ref, routes_hbm, modality_hbm, router_hbm, w_in_ref, w_out_ref,
     mixed_ref, load_ref,
-    routes_ref, modality_ref, router_ref, win, wout, tok_buf, placer, gate, buffer, rows, hidden, served, returned,
+    routes_ref, modality_ref, router_ref, win, wout, tok_buf, placer, gate, buffer, rows, hidden, partial, served, returned,
     stat, stat_rx, stat_sum, stat_rx2,
     tok_sem, local_sem, ring_send, ring_recv, pair_send, pair_recv,
     disp_send, disp_recv, back_send, back_recv, stat_send, stat_recv, row_in, cross_send, cross_recv,
@@ -273,8 +273,18 @@
             placer[...], returned[n][...], preferred_element_type=jnp.float32)
         mixed_ref[:, columns(n)] = (combined * gate[:, 0:1]).astype(jnp.bfloat16)
 
+    far_side = lax.rem(z + NZ // 2, NZ) // (NZ // 2)
+    half_ff = hidden.shape[1] // 2
+
+    def half_product(n, side):
+        at = pl.ds(pl.multiple_of(side * half_ff, 128), half_ff)
+        return jnp.dot(hidden[:, at], wout[n][at, :], preferred_element_type=jnp.float32)
+
+    def second_product_start(n):
+        partial[:, pl.ds(0, WIDTHS_OUT[n])] = half_product(n, 1 - far_side)
+
     def second_product(n):
-        acc = jnp.dot(hidden[...], wout[n][...], preferred_element_type=jnp.float32)
+        acc = partial[:, pl.ds(0, WIDTHS_OUT[n])] + half_product(n, far_side)
         served[n][...] = acc.astype(jnp.bfloat16)
         returned[n][own_rows, :] = served[n][own_rows, :]
         send_back(n)
@@ -282,9 +292,8 @@
             combine(n - 2)
 
     def product(n):
-        for (direction, hop) in pair_slots():
-            if n < chunks - 1 or hop < last:
-                pair_copy(n, direction, hop, other).wait_recv()
+        if n < chunks - 1:
+            pair_copy(n, 0, last, other).wait_recv()
         if n == chunks - 1:
             for direction in range(2):
                 cross_copy(n, direction, other, last).wait_recv()
@@ -309,6 +318,10 @@
                 pair_copy(n, direction, hop, c).start()
         n = r - last
         if n >= 0:
+            for (direction, hop) in pair_slots()[:-1]:
+                pair_copy(n, direction, hop, other).wait_recv()
+            if n >= CHUNKS_IN:
+                second_product_start(n - CHUNKS_IN)
             for direction in range(2):
                 ring_arrival(n, direction, last).wait_recv()
             if n < chunks - 1:
@@ -388,6 +401,7 @@
             pltpu.VMEM((slots, model_width), bf16),
             pltpu.VMEM((slots, model_width), bf16),
             pltpu.VMEM((slots, ff), bf16),
+            pltpu.VMEM((slots, max(WIDTHS_OUT)), f32),
             [pltpu.VMEM((slots, w), bf16) for w in WIDTHS_OUT],
             [pltpu.VMEM((slots, w), bf16) for w in WIDTHS_OUT],
             pltpu.VMEM((experts, 128), f32),

time: 153 us -> 152 us (level)
  no operation moved by 1% of the time
where the time goes in v5:
time: 152 us; the launch traced here: 151 us
  Pallas kernels  149 us (98%)
    pallas_call x1, Pallas kernels, on_device(): pl.pallas_call(layer_kernel, out_shape=(pltpu.VMEM((toks, model_width), b...  149 us

profile of v5, /device:TPU:1, one launch (start us, length us, event | category | flops | bytes accessed | tf_op | source)
XLA Modules:
  0.0 151.4 jit_solution(16181807674927446506)
XLA Ops:
  0.6 149.3 %layer.1 = (bf16[256,1280]{1,0:T(8,128)(2,1)S(1)}, f32[2,2,16]{2,1,0:T(2,128)S(1)}) custom-call(bf16[256,1280]{1,0:T(8,128)(2,1)} %bitcast.5, s32[2,1,128]{2,1,0:T(1,128)} %bitcast.7, s32[2,128]{1,0:T(2,128)} %modality_hbm.1, bf16[16,1280]{1,0:T(8,128)(2,1)} %bitcast.6, bf16[1,80,5120]{2,1,0:T(8,128)(2,1)} %w_in_ref.1, bf16[1,320,1280]{2,1,0:T(8,128)(2,1)} %w_out_ref.1), custom_call_target="tpu_custom_call" | custom-call | tf_op jit(solution)/shard_map/layer/pallas_call | solution.py:384
  150.0 0.8 copy.10
  150.8 0.6 copy.11

commit v6 on v5

--- a/solution.py
+++ b/solution.py
@@ -364,6 +364,17 @@
     combine(CHUNKS_OUT - 1)
     for n in range(CHUNKS_OUT):
         take(served[n].at[pl.ds(0, others)], back_send.at[n])
+
+
+def hand_over(mixed_ref, load_ref, mixed_out, load_out, sem):
+    copies = [
+        pltpu.make_async_copy(mixed_ref, mixed_out, sem.at[0]),
+        pltpu.make_async_copy(load_ref, load_out, sem.at[1]),
+    ]
+    for copy in copies:
+        copy.start()
+    for copy in copies:
+        copy.wait()
 
 
 def on_device(tokens, modality, routes, router, w_in, w_out):
@@ -436,6 +447,18 @@
         w_in,
         w_out,
     )
+    mixed, load = pl.pallas_call(
+        hand_over,
+        out_shape=(
+            jax.ShapeDtypeStruct((toks, model_width), bf16),
+            jax.ShapeDtypeStruct((2, 2, experts), f32),
+        ),
+        in_specs=[vmem, vmem],
+        out_specs=(hbm, hbm),
+        scratch_shapes=[dma((2,))],
+        compiler_params=pltpu.CompilerParams(vmem_limit_bytes=4 * 1024 * 1024),
+        name="hand_over",
+    )(mixed, load)
     return mixed.reshape(tokens.shape), load
 
 

time: 152 us -> 151 us (level)
  no operation moved by 1% of the time
where the time goes in v6:
time: 151 us
  Pallas kernels  150 us (99%)
    pallas_call x1, Pallas kernels, on_device(): pl.pallas_call(layer_kernel, out_shape=(pltpu.VMEM((toks, model_width), b...  149 us

profile of v6, /device:TPU:1, one launch (start us, length us, event | category | flops | bytes accessed | tf_op | source)
XLA Modules:
  0.0 150.8 jit_solution(450785872238736029)
XLA Ops:
  0.6 149.3 %layer.1 = (bf16[256,1280]{1,0:T(8,128)(2,1)S(1)}, f32[2,2,16]{2,1,0:T(2,128)S(1)}) custom-call(bf16[256,1280]{1,0:T(8,128)(2,1)} %bitcast.4, s32[2,1,128]{2,1,0:T(1,128)} %bitcast.6, s32[2,128]{1,0:T(2,128)} %modality_hbm.1, bf16[16,1280]{1,0:T(8,128)(2,1)} %bitcast.5, bf16[1,80,5120]{2,1,0:T(8,128)(2,1)} %w_in_ref.1, bf16[1,320,1280]{2,1,0:T(8,128)(2,1)} %w_out_ref.1), custom_call_target="tpu_custom_call" | custom-call | tf_op jit(solution)/shard_map/layer/pallas_call | solution.py:395
  150.0 0.9 hand_over.1
